TPU v7x, 32 devices: a whole 2x2x4 slice. The times are simulated.
32 devices in a mesh: grp: 4 (over y, x), grid: 8 (over z, core).
Axes of the slice: x: 2, y: 2, z: 4, core: 2. Of those that a mesh axis runs over, the one named last changes fastest.
Arguments:
- orbitals: float32 [64, 262144], P('grp', 'grid'), may hold values from -6 to 6
- anchors: int32 [64, 3], replicated, may hold values from 0 to 31
- pair_slots: int32 [32, 4, 2], replicated, may hold values from -1 to 63, as said below
Outputs:
- exchange_term: float32 [64, 262144], P('grp', 'grid')
Inputs may be any that keep to these rules, and one draw needn't show every extreme that they name: `pair_slots`: row k lists the pairs of owner k, the device with index k in the order grp, grid; its first slots hold pairs of two different orbital numbers and its other slots hold -1 in both columns. Exactly 64 slots hold pairs in all, no row holds more than 4, and some row holds exactly 4.
All inputs are finite; a program needn't handle non-finite values.
Results may differ from a plain program's by a relative error of at most 0.0003.
Values sent between devices are 32-bit elements; how exact they have to be, the bound alone decides.
A program may use at most 128 MiB of HBM per device.

v0:
```python
import jax
import jax.numpy as jnp
from jax import lax
from jax.sharding import PartitionSpec as P

B = 64
PAIR_DEV = 2
ITERS = 3


def shift_field(field, offset, extent):
    plane_size = extent * extent
    padded_x = jnp.pad(field, ((extent, extent), (0, 0)))
    moved = lax.dynamic_slice_in_dim(padded_x, extent - offset[0], extent, 0)
    padded_yz = jnp.pad(moved, ((0, 0), (plane_size, plane_size)))
    linear = offset[1] * extent + offset[2]
    moved = lax.dynamic_slice_in_dim(padded_yz, plane_size - linear, plane_size, 1)
    cells = lax.broadcasted_iota(jnp.int32, (1, plane_size), 1)
    coord_y = cells // extent - offset[1]
    coord_z = cells % extent - offset[2]
    inside = (coord_y >= 0) & (coord_y < extent) & (coord_z >= 0) & (coord_z < extent)
    return jnp.where(inside, moved, jnp.zeros_like(moved))


def operate(field, extent):
    padded_x = jnp.pad(field, ((1, 1), (0, 0)))
    beside = padded_x[2:] + padded_x[:-2]
    padded_y = jnp.pad(field, ((0, 0), (extent, extent)))
    beside = beside + padded_y[:, 2 * extent :] + padded_y[:, : -2 * extent]
    padded_z = jnp.pad(field, ((0, 0), (1, 1)))
    cells = lax.broadcasted_iota(jnp.int32, (1, field.shape[1]), 1) % extent
    upper_z = jnp.where(cells < extent - 1, padded_z[:, 2:], jnp.zeros_like(field))
    lower_z = jnp.where(cells > 0, padded_z[:, :-2], jnp.zeros_like(field))
    return 6.0 * field - beside - upper_z - lower_z


def conjugate(density, extent):
    potential = jnp.zeros_like(density)
    resid = density
    direction = density
    norm_now = jnp.sum(resid * resid)
    for turn in range(ITERS):
        image = operate(direction, extent)
        step_len = norm_now / jnp.sum(direction * image)
        potential = potential + step_len * direction
        resid = resid - step_len * image
        norm_next = jnp.sum(resid * resid)
        direction = resid + norm_next / norm_now * direction
        norm_now = norm_next
    return potential


def pair_terms(field_a, field_b, offset, extent):
    partner = shift_field(field_b, offset, extent)
    density = field_a * partner
    potential = conjugate(density, extent)
    term_a = potential * partner
    term_b = shift_field(potential * field_a, -offset, extent)
    return (term_a, term_b)


def deal_evenly(pair_slots, owner_count, each_owner):
    flat_slots = pair_slots.reshape(-1, 2)
    filled = (flat_slots[:, 0] >= 0).astype(jnp.int32)
    position = jnp.cumsum(filled, dtype=jnp.int32) - filled
    wanted = lax.broadcasted_iota(jnp.int32, (owner_count, each_owner), 1) * owner_count
    wanted = (wanted + lax.broadcasted_iota(jnp.int32, (owner_count, each_owner), 0)).reshape(-1)
    matched = (position[None, :] == wanted[:, None]) & (filled[None, :] == 1)
    picked = jnp.dot(matched.astype(jnp.int32), flat_slots)
    return picked.reshape(owner_count, each_owner, 2)


def body(orbitals, anchors, pair_slots):
    extent = B
    grid_count = lax.axis_size("grid")
    owner_count = lax.axis_size("grp") * grid_count
    group_idx = lax.axis_index("grp")
    place_idx = lax.axis_index("grid")
    assignment = deal_evenly(pair_slots, owner_count, PAIR_DEV)
    slot_count = assignment.shape[1]
    filled = assignment[..., 0] >= 0
    safe_ids = jnp.maximum(assignment, 0)
    pieces = lax.all_gather(orbitals, "grp", axis=0, tiled=True)
    group_table = lax.dynamic_slice_in_dim(safe_ids, group_idx * grid_count, grid_count, 0)
    gather_ids = jnp.transpose(group_table, (1, 2, 0))
    outgoing = pieces[gather_ids]
    arrived = lax.all_to_all(outgoing, "grid", split_axis=2, concat_axis=2, tiled=True)
    boxes = arrived.reshape(slot_count, 2, extent, extent * extent)
    owner_idx = group_idx * grid_count + place_idx
    own_pairs = safe_ids[owner_idx]
    own_filled = filled[owner_idx]
    offsets = anchors[own_pairs[:, 1]] - anchors[own_pairs[:, 0]]

    def solve_slot(slot_item):
        boxes_pair, offset, flag = slot_item
        term_a, term_b = pair_terms(boxes_pair[0], boxes_pair[1], offset, extent)
        weight_flag = jnp.where(flag, 1.0, 0.0).astype(jnp.float32)
        return jnp.stack([term_a, term_b]) * weight_flag

    terms = lax.map(solve_slot, (boxes, offsets, own_filled))
    returned = lax.all_to_all(
        terms.reshape(slot_count, 2, grid_count, -1),
        "grid",
        split_axis=2,
        concat_axis=2,
        tiled=True,
    )
    flat_terms = returned.reshape(-1, returned.shape[-1])
    summed = jax.ops.segment_sum(flat_terms, gather_ids.reshape(-1), num_segments=anchors.shape[0])
    return lax.psum_scatter(summed, "grp", scatter_dimension=0, tiled=True)


def solution(mesh):
    return jax.shard_map(
        body,
        mesh=mesh,
        in_specs=(P("grp", "grid"), P(), P()),
        out_specs=P("grp", "grid"),
        check_vma=False,
    )
```

profile of v0, /device:TPU:0, one launch (start us, length us, event | category | flops | bytes accessed | tf_op | source)
XLA Modules:
  0.0 509.3 jit_solution(14262574383303529083)
XLA Ops:
  6.5 0.7 all-gather.2.cloned.1.call-update
  7.3 0.8 copy.17
  9.0 90.4 %all-gather.2.cloned.1.call-done = f32[64,32768]{1,0:T(8,128)} async-done(((f32[16,32768]{1,0:T(8,128)}), f32[64,32768]{1,0:T(8,128)}) %all-gather.2.cloned.1.call-update) | async-done | bytes 8388624 | tf_op jit(solution)/shard_map/all_gather | solution.py:83
  99.4 8.8 %gather_fusion = f32[32,32768]{1,0:T(8,128)} fusion(f32[64,32768]{1,0:T(8,128)} %all-gather.2.cloned.1.call-done, s32[1024]{0:T(1024)S(1)} %pad_clamp_fusion.2), kind=kCustom, calls=%fused_computation | custom fusion | bytes 8388736 | tf_op jit(solution)/shard_map/gather | solution.py:86
  108.2 7.4 %copy.19 = f32[2,2,8,32768]{3,1,0,2:T(2,128)} copy(f32[2,2,8,32768]{3,2,1,0:T(8,128)} %bitcast.60) | data formatting | bytes 8388608 | tf_op jit(solution)/shard_map/gather | solution.py:86
  115.6 4.9 all-to-all-start
  121.0 0.6 gather_fusion.2
  121.6 0.6 gather_fusion.1
  122.3 92.1 %all-to-all-done = f32[2,2,8,32768]{3,1,0,2:T(2,128)} async-done(((f32[2,2,8,32768]{3,1,0,2:T(2,128)}), f32[2,2,8,32768]{3,1,0,2:T(2,128)}, u32[]{:S(2)}, u32[]{:S(2)}) %all-to-all-start) | async-done | bytes 4194336 | tf_op jit(solution)/shard_map/all_to_all | solution.py:87
  214.4 6.6 %copy.20 = f32[2,2,8,32768]{3,2,1,0:T(8,128)} copy(f32[2,2,8,32768]{3,1,0,2:T(2,128)} %all-to-all-done) | data formatting | bytes 8388608 | tf_op jit(solution)/shard_map/all_to_all | solution.py:87
  221.0 4.9 reshape.254
  226.0 64.2 %while.13 = (s32[]{:T(128)}, f32[2,2,64,4096]{3,2,1,0:T(8,128)}, f32[2,2,64,4096]{3,2,1,0:T(8,128)}, s32[2,3]{1,0:T(2,128)S(1)}, pred[2]{0:T(512)(128)(4,1)S(1)}...) while((s32[]{:T(128)}, f32[2,2,64,4096]{3,2,1,0:T(8,128)}, ...), condition=%wide.region_8.9_spmd, body=%wide.region_1.8_spmd.sunk | while | flops 22224920 | bytes 80794384 | solution.py:100
  226.0 0.6 dynamic_slice.96
  227.2 0.6 fusion.80
  232.8 1.2 fusion.85
  234.0 1.2 fusion.81
  235.3 1.3 dynamic-slice_bitcast_fusion.5
  236.7 1.0 copy-done
  237.7 1.6 fusion.82
  239.3 1.8 multiply_reduce_fusion.9
  242.3 0.9 multiply_reduce_fusion.10
  244.6 1.8 multiply_reduce_fusion.11
  247.6 0.9 multiply_reduce_fusion.12
  250.0 1.8 fusion.84
  253.0 2.3 multiply_bitcast_fusion.2
  255.5 0.3 fusion.86
  256.1 2.0 copy-done.2
  258.0 0.6 dynamic_slice.96
  259.3 0.6 fusion.80
  264.9 1.2 fusion.85
  266.1 1.2 fusion.81
  267.4 1.3 dynamic-slice_bitcast_fusion.5
  268.8 1.0 copy-done
  269.8 1.6 fusion.82
  271.4 1.8 multiply_reduce_fusion.9
  274.4 0.9 multiply_reduce_fusion.10
  276.7 1.8 multiply_reduce_fusion.11
  279.7 0.9 multiply_reduce_fusion.12
  282.1 1.8 fusion.84
  285.1 2.3 multiply_bitcast_fusion.2
  288.2 2.0 copy-done.2
  290.1 4.9 reshape.255
  295.1 7.4 %copy.23 = f32[2,2,8,32768]{3,1,0,2:T(2,128)} copy(f32[2,2,8,32768]{3,2,1,0:T(8,128)} %reshape.255) | data formatting | bytes 8388608 | tf_op jit(solution)/shard_map/reshape | solution.py:102
  302.5 4.5 all-to-all-start.1
  307.1 93.8 %all-to-all-done.1 = f32[2,2,8,32768]{3,1,0,2:T(2,128)} async-done(((f32[2,2,8,32768]{3,1,0,2:T(2,128)}), f32[2,2,8,32768]{3,1,0,2:T(2,128)}, u32[]{:S(2)}, u32[]{:S(2)}) %all-to-all-start.1) | async-done | bytes 4194336 | tf_op jit(solution)/shard_map/all_to_all | solution.py:101
  401.0 6.6 %copy.24 = f32[2,2,8,32768]{3,2,1,0:T(8,128)} copy(f32[2,2,8,32768]{3,1,0,2:T(2,128)} %all-to-all-done.1) | data formatting | bytes 8388608 | tf_op jit(solution)/shard_map/all_to_all | solution.py:101
  407.6 10.4 %scatter_custom_fusion = f32[64,32768]{1,0:T(8,128)} fusion(s32[32]{0:T(128)S(1)} %reshape.283, f32[32,32768]{1,0:T(8,128)} %bitcast.61, f32[]{:T(128)} %constant.162.clone.1), kind=kCustom, calls=%fused_computation.86 | custom fusion | flops 1048576 | bytes 8389120 | tf_op jit(solution)/shard_map/scatter-add | solution.py:109
  418.0 84.5 %reduce-scatter.2.cloned.1.call-done = f32[16,32768]{1,0:T(8,128)} async-done(((f32[64,32768]{1,0:T(8,128)}), f32[16,32768]{1,0:T(8,128)}) %reduce-scatter.2.cloned.1.call-update) | async-done | bytes 2097168 | tf_op jit(solution)/shard_map/reduce_scatter | solution.py:110
  (46 shorter events, 4.0 us)
Async XLA Ops:
  6.5 92.9 %all-gather.2.cloned.1.call-start = ((), (), s32[]{:S(2)}) async-start(), calls=%async_computation.3 | async-start | bytes 10485760 | tf_op jit(solution)/shard_map/all_gather | solution.py:83
  115.6 4.9 copy-start.3
  115.6 98.8 %all-to-all-start = ((f32[2,2,8,32768]{3,1,0,2:T(2,128)}), f32[2,2,8,32768]{3,1,0,2:T(2,128)}, u32[]{:S(2)}, u32[]{:S(2)}) async-start(f32[2,2,8,32768]{3,1,0,2:T(2,128)} %copy.19), calls=%async_computation | async-start | bytes 8388608 | tf_op jit(solution)/shard_map/all_to_all | solution.py:87
  236.7 1.0 copy-start
  253.0 2.8 copy-start.1
  256.1 2.0 copy-start.2
  268.8 1.0 copy-start
  285.1 2.8 copy-start.1
  288.2 2.0 copy-start.2
  302.5 98.5 %all-to-all-start.1 = ((f32[2,2,8,32768]{3,1,0,2:T(2,128)}), f32[2,2,8,32768]{3,1,0,2:T(2,128)}, u32[]{:S(2)}, u32[]{:S(2)}) async-start(f32[2,2,8,32768]{3,1,0,2:T(2,128)} %copy.23), calls=%async_computation.1 | async-start | bytes 8388608 | tf_op jit(solution)/shard_map/all_to_all | solution.py:101
  307.0 195.4 %reduce-scatter.2.cloned.1.call-start = ((), (), s32[]{:S(2)}) async-start(), calls=%async_computation.4 | async-start | bytes 10485760 | tf_op jit(solution)/shard_map/reduce_scatter | solution.py:110
Sparse Core Ops, SparseCore 0:
  9.2 90.1 all-gather.1
  418.1 84.2 reduce-scatter.1
where the time goes:
time: 511 us; the launch traced here: 509 us
  waiting for transfers between devices  362 us (71%)
  local copies, waits for them, and re-layouts  60.4 us (12%)
  other arithmetic  40.1 us (8%)
  loops' own time  24.1 us (5%)
  between operations  13.5 us (3%)
  starting transfers between devices  9.44 us (2%)
    all_to_all x1, waiting for transfers between devices, body(): lax.all_to_all(terms.reshape(slot_count, 2, grid_count, -1), 'grid', spli...  93.8 us
    all_to_all x1, waiting for transfers between devices, body(): lax.all_to_all(outgoing, 'grid', split_axis=2, concat_axis=2, tiled=True)  92.1 us
    all_gather x1, waiting for transfers between devices, body(): pieces = lax.all_gather(orbitals, 'grp', axis=0, tiled=True)  90.4 us
    reduce_scatter x1, waiting for transfers between devices, body(): return lax.psum_scatter(summed, 'grp', scatter_dimension=0, tiled=True)  84.5 us
    another operation x1, loops' own time, body(): terms = lax.map(solve_slot, (boxes, offsets, own_filled))  24.1 us
    gather x2, local copies, waits for them, and re-layouts, body(): outgoing = pieces[gather_ids]  16.2 us
    reshape x2, local copies, waits for them, and re-layouts, body(): terms.reshape(slot_count, 2, grid_count, -1)  12.3 us
    reduce_sum x6, other arithmetic, conjugate(): step_len = norm_now / jnp.sum(direction * image)  10.6 us
  transfers between devices with their start and end apart: 4, of which 4 were waited for; matrix products, arithmetic and copies ran while one was open for 1% of the time, Pallas kernels for 0%

commit v1 on v0

v1 whole, which is shorter than its diff:
```python
import math

import jax
import jax.numpy as jnp
from jax import lax
from jax.experimental import pallas as pl
from jax.experimental.pallas import tpu as pltpu
from jax.sharding import PartitionSpec as P

B = 64
PAIR_DEV = 2
ITERS = 3
MOST_CHUNKS = 2
LANES = 128
ROWS = B * B // LANES
PAD = 32
STEP = 4


def deal_evenly(pair_slots, owner_count, each_owner):
    flat_slots = pair_slots.reshape(-1, 2)
    filled = (flat_slots[:, 0] >= 0).astype(jnp.int32)
    position = jnp.cumsum(filled, dtype=jnp.int32) - filled
    wanted = lax.broadcasted_iota(jnp.int32, (owner_count, each_owner), 1) * owner_count
    wanted = (wanted + lax.broadcasted_iota(jnp.int32, (owner_count, each_owner), 0)).reshape(-1)
    matched = (position[None, :] == wanted[:, None]) & (filled[None, :] == 1)
    picked = jnp.sum(jnp.where(matched[:, :, None], flat_slots[None], 0), axis=1)
    return picked.reshape(owner_count, each_owner, 2)


def gather_kernel(ids_ref, src_ref, *out_refs):
    count, terms = out_refs[0].shape[:2]
    for slot, out_ref in enumerate(out_refs):
        def pick(dest, unused, slot=slot, out_ref=out_ref):
            for term in range(terms):
                out_ref[dest, term] = src_ref[ids_ref[(slot * count + dest) * terms + term]]
            return unused

        lax.fori_loop(0, count, pick, 0)


def gather_pieces(ids, pieces, slots, count):
    norb, rows, lanes = pieces.shape
    block = max(8, rows // 4)
    return pl.pallas_call(
        gather_kernel,
        grid_spec=pltpu.PrefetchScalarGridSpec(
            num_scalar_prefetch=1,
            grid=(rows // block,),
            in_specs=[pl.BlockSpec((norb, block, lanes), lambda i, ids: (0, i, 0))],
            out_specs=[pl.BlockSpec((count, 2, block, lanes), lambda i, ids: (0, 0, i, 0))] * slots,
        ),
        out_shape=[jax.ShapeDtypeStruct((count, 2, rows, lanes), jnp.float32)] * slots,
        cost_estimate=pl.CostEstimate(flops=0, bytes_accessed=8 * norb * rows * lanes, transcendentals=0),
        name="pick_pieces",
    )(ids, pieces)


def scatter_kernel(ids_ref, *refs):
    out_ref = refs[-1]
    out_ref[...] = jnp.zeros_like(out_ref)
    count, terms = refs[0].shape[:2]
    for slot, in_ref in enumerate(refs[:-1]):
        def add(dest, unused, slot=slot, in_ref=in_ref):
            for term in range(terms):
                orbit = ids_ref[(slot * count + dest) * terms + term]
                out_ref[orbit] = out_ref[orbit] + in_ref[dest, term]
            return unused

        lax.fori_loop(0, count, add, 0)


def scatter_pieces(ids, parts, norb):
    count, terms, rows, lanes = parts[0].shape
    block = max(8, rows // 4)
    return pl.pallas_call(
        scatter_kernel,
        grid_spec=pltpu.PrefetchScalarGridSpec(
            num_scalar_prefetch=1,
            grid=(rows // block,),
            in_specs=[pl.BlockSpec((count, terms, block, lanes), lambda i, ids: (0, 0, i, 0))] * len(parts),
            out_specs=pl.BlockSpec((norb, block, lanes), lambda i, ids: (0, i, 0)),
        ),
        out_shape=jax.ShapeDtypeStruct((norb, rows, lanes), jnp.float32),
        cost_estimate=pl.CostEstimate(flops=0, bytes_accessed=8 * norb * rows * lanes, transcendentals=0),
        name="add_pieces",
    )(ids, *parts)


def lane_ids(shape):
    return lax.broadcasted_iota(jnp.int32, shape, len(shape) - 1)


def shift_plane(plane, off_y, off_z):
    shape = plane.shape
    lane = lane_ids(shape)
    row = lax.broadcasted_iota(jnp.int32, shape, 0)
    linear = off_y * B + off_z
    across = jnp.bitwise_and(linear, LANES - 1)
    down = jnp.right_shift(linear, 7)
    turned = pltpu.roll(plane, across, 1)
    near = pltpu.roll(turned, jnp.bitwise_and(down, ROWS - 1), 0)
    far = pltpu.roll(turned, jnp.bitwise_and(down + 1, ROWS - 1), 0)
    moved = jnp.where(lane >= across, near, far)
    from_y = row * 2 + jnp.right_shift(lane, 6) - off_y
    from_z = jnp.bitwise_and(lane, B - 1) - off_z
    inside = (from_y >= 0) & (from_y < B) & (from_z >= 0) & (from_z < B)
    return jnp.where(inside, moved, 0.0)


def operate_plane(before, plane, after):
    shape = plane.shape
    lane = lane_ids(shape)
    row = lax.broadcasted_iota(jnp.int32, shape, 0)
    z = jnp.bitwise_and(lane, B - 1)
    upper_z = jnp.where(z < B - 1, pltpu.roll(plane, LANES - 1, 1), 0.0)
    lower_z = jnp.where(z > 0, pltpu.roll(plane, 1, 1), 0.0)
    half = pltpu.roll(plane, B, 1)
    down = jnp.where(row > 0, pltpu.roll(half, 1, 0), 0.0)
    up = jnp.where(row < ROWS - 1, pltpu.roll(half, ROWS - 1, 0), 0.0)
    beside = (before + after) + (half + jnp.where(lane < B, down, up))
    return 6.0 * plane - beside - upper_z - lower_z


def fold(values):
    return jnp.sum(values.reshape(ROWS // 8, 8, LANES), axis=0)


def total(acc):
    return jnp.sum(acc, axis=(0, 1), keepdims=True)


def solve_kernel(info_ref, *refs):
    chunks = (len(refs) - 6) // 2
    in_refs, out_refs = refs[:chunks], refs[chunks : 2 * chunks]
    wide, partner, direction, resid, image, potential = refs[2 * chunks :]
    count, terms, rows, lanes = in_refs[0].shape
    each = rows // ROWS
    dx, dy, dz = info_ref[0], info_ref[1], info_ref[2]
    keep = jnp.where(info_ref[3] > 0, 1.0, 0.0).astype(jnp.float32)
    edge = jnp.zeros((PAD, ROWS, LANES), jnp.float32)
    wide[pl.ds(0, PAD)] = edge
    wide[pl.ds(PAD + B, PAD)] = edge
    direction[0] = edge[0]
    direction[B + 1] = edge[0]
    none = jnp.zeros((8, LANES), jnp.float32)

    def place(owner, chunk, i):
        return (owner * chunks + chunk) * each + i

    def load(owner, unused):
        for chunk in range(chunks):
            for i in range(each):
                wide[PAD + place(owner, chunk, i)] = in_refs[chunk][owner, 1, pl.ds(i * ROWS, ROWS)]
        return unused

    lax.fori_loop(0, count, load, 0)

    def start(owner, acc):
        for chunk in range(chunks):
            for i in range(each):
                x = place(owner, chunk, i)
                other = shift_plane(wide[PAD + x - dx], dy, dz)
                partner[x] = other
                density = in_refs[chunk][owner, 0, pl.ds(i * ROWS, ROWS)] * other
                direction[x + 1] = density
                resid[x] = density
                acc = acc + fold(density * density)
        return acc

    norm_now = total(lax.fori_loop(0, count, start, none))

    for turn in range(ITERS):
        def apply(block, acc):
            for i in range(STEP):
                x = block * STEP + i
                plane = direction[x + 1]
                result = operate_plane(direction[x], plane, direction[x + 2])
                image[x] = result
                acc = acc + fold(plane * result)
            return acc

        step_len = norm_now / total(lax.fori_loop(0, B // STEP, apply, none))

        if turn == ITERS - 1:
            break

        def advance(block, acc):
            for i in range(STEP):
                x = block * STEP + i
                moved = step_len * direction[x + 1]
                potential[x] = moved if turn == 0 else potential[x] + moved
                left = resid[x] - step_len * image[x]
                resid[x] = left
                acc = acc + fold(left * left)
            return acc

        norm_next = total(lax.fori_loop(0, B // STEP, advance, none))
        ratio = norm_next / norm_now

        def renew(block, unused):
            for i in range(STEP):
                x = block * STEP + i
                direction[x + 1] = resid[x] + ratio * direction[x + 1]
            return unused

        lax.fori_loop(0, B // STEP, renew, 0)
        norm_now = norm_next

    def finish(owner, unused):
        for chunk in range(chunks):
            for i in range(each):
                x = place(owner, chunk, i)
                found = (potential[x] + step_len * direction[x + 1]) * keep
                out_refs[chunk][owner, 0, pl.ds(i * ROWS, ROWS)] = found * partner[x]
                wide[PAD + x] = found * in_refs[chunk][owner, 0, pl.ds(i * ROWS, ROWS)]
        return unused

    lax.fori_loop(0, count, finish, 0)

    def give_back(owner, unused):
        for chunk in range(chunks):
            for i in range(each):
                x = place(owner, chunk, i)
                out_refs[chunk][owner, 1, pl.ds(i * ROWS, ROWS)] = shift_plane(wide[PAD + x + dx], -dy, -dz)
        return unused

    lax.fori_loop(0, count, give_back, 0)


def solve_pair(info, parts):
    box = (B, ROWS, LANES)
    vmem = pl.BlockSpec(memory_space=pltpu.VMEM)
    return pl.pallas_call(
        solve_kernel,
        in_specs=[pl.BlockSpec(memory_space=pltpu.SMEM)] + [vmem] * len(parts),
        out_specs=[vmem] * len(parts),
        out_shape=[jax.ShapeDtypeStruct(p.shape, jnp.float32) for p in parts],
        scratch_shapes=[
            pltpu.VMEM((B + 2 * PAD, ROWS, LANES), jnp.float32),
            pltpu.VMEM(box, jnp.float32),
            pltpu.VMEM((B + 2, ROWS, LANES), jnp.float32),
            pltpu.VMEM(box, jnp.float32),
            pltpu.VMEM(box, jnp.float32),
            pltpu.VMEM(box, jnp.float32),
        ],
        compiler_params=pltpu.CompilerParams(vmem_limit_bytes=32 * 1024 * 1024),
        cost_estimate=pl.CostEstimate(flops=0, bytes_accessed=40 * 1024 * 1024, transcendentals=0),
        name="solve_pair",
    )(info, *parts)


def body(orbitals, anchors, pair_slots):
    grid_count = lax.axis_size("grid")
    owner_count = lax.axis_size("grp") * grid_count
    group_idx = lax.axis_index("grp")
    place_idx = lax.axis_index("grid")
    assignment = deal_evenly(pair_slots, owner_count, PAIR_DEV)
    slots = assignment.shape[1]
    filled = assignment[..., 0] >= 0
    safe_ids = jnp.maximum(assignment, 0)
    group_table = lax.dynamic_slice_in_dim(safe_ids, group_idx * grid_count, grid_count, 0)
    ids = jnp.transpose(group_table, (1, 0, 2)).reshape(-1)
    owner_idx = group_idx * grid_count + place_idx
    own_pairs = safe_ids[owner_idx]
    offsets = anchors[own_pairs[:, 1]] - anchors[own_pairs[:, 0]]
    info = jnp.concatenate([offsets, filled[owner_idx].astype(jnp.int32)[:, None]], axis=1)

    norb_local, cells = orbitals.shape
    stacked = orbitals.reshape(norb_local, cells // LANES, LANES)
    chunks = math.gcd(MOST_CHUNKS, cells // (B * B))
    rows = stacked.shape[1] // chunks
    arrived = [[None] * chunks for _ in range(slots)]
    for chunk in range(chunks):
        pieces = lax.all_gather(stacked[:, chunk * rows : (chunk + 1) * rows], "grp", axis=0, tiled=True)
        outgoing = gather_pieces(ids, pieces, slots, grid_count)
        for slot in range(slots):
            arrived[slot][chunk] = lax.all_to_all(outgoing[slot], "grid", split_axis=0, concat_axis=0, tiled=True)
    returned = []
    for slot in range(slots):
        terms = solve_pair(info[slot], arrived[slot])
        returned.append(
            [lax.all_to_all(t, "grid", split_axis=0, concat_axis=0, tiled=True) for t in terms]
        )
    results = []
    for chunk in range(chunks):
        summed = scatter_pieces(ids, [r[chunk] for r in returned], anchors.shape[0])
        results.append(lax.psum_scatter(summed, "grp", scatter_dimension=0, tiled=True))
    return jnp.concatenate(results, axis=1).reshape(norb_local, cells)


def solution(mesh):
    return jax.shard_map(
        body,
        mesh=mesh,
        in_specs=(P("grp", "grid"), P(), P()),
        out_specs=P("grp", "grid"),
        check_vma=False,
    )
```

time: 511 us -> 388 us (0.76)
  waiting for transfers between devices: 362 us -> 152 us
  blocking collectives: 0 us -> 152 us
  local copies, waits for them, and re-layouts: 60.4 us -> 14 us
  Pallas kernels: 0 us -> 42 us
  other arithmetic: 40.1 us -> 2.59 us
  loops' own time: 24.1 us -> 0 us
    all_to_all x2 -> x3, waiting for transfers between devices: 186 us -> 32.7 us  [the longest x2 17.8 us: body(): lax.all_to_all(outgoing[slot], 'grid', split_axis=0, concat_axis=0, tiled...]
    all_to_all x0 -> x5, blocking collectives: none -> 152 us  [the longest x3 90.1 us: body(): lax.all_to_all(t, 'grid', split_axis=0, concat_axis=0, tiled=True)]
    pallas_call x0 -> x6, Pallas kernels: none -> 42 us  [the longest x2 21.2 us: solve_pair(): pl.pallas_call(solve_kernel, in_specs=[pl.BlockSpec(memory_space=pltpu.SM...]
    reduce_scatter x1 -> x2, waiting for transfers between devices: 84.5 us -> 50.7 us  [body(): lax.psum_scatter(summed, 'grp', scatter_dimension=0, tiled=True)]
    another operation x1 -> x0, loops' own time: 24.1 us -> none  [body(): terms = lax.map(solve_slot, (boxes, offsets, own_filled))]
    all_gather x1 -> x2, waiting for transfers between devices: 90.4 us -> 67.5 us  [body(): lax.all_gather(stacked[:, chunk * rows:(chunk + 1) * rows], 'grp', axis=0...]
    reshape x3, local copies, waits for them, and re-layouts: 17.3 us -> 0.82 us  [the longest x1 0.66 us: body(): ids = jnp.transpose(group_table, (1, 0, 2)).reshape(-1)]
    gather x2 -> x0, local copies, waits for them, and re-layouts: 16.2 us -> none  [body(): outgoing = pieces[gather_ids]]
  transfers between devices with their start and end apart: 4 -> 7, of which waited for: 4 -> 6; matrix products, arithmetic and copies ran while one was open for 1% -> 1% of each run, Pallas kernels for 0% -> 9%
where the time goes in v1:
time: 388 us; the launch traced here: 387 us
  waiting for transfers between devices  152 us (39%)
  blocking collectives  152 us (39%)
  Pallas kernels  42 us (11%)
  local copies, waits for them, and re-layouts  14 us (4%)
  between operations  13.3 us (3%)
  starting transfers between devices  11.5 us (3%)
    all_to_all x3, blocking collectives, body(): lax.all_to_all(t, 'grid', split_axis=0, concat_axis=0, tiled=True)  90.1 us
    all_gather x2, waiting for transfers between devices, body(): lax.all_gather(stacked[:, chunk * rows:(chunk + 1) * rows], 'grp', axis=0...  67.5 us
    all_to_all x2, blocking collectives, body(): lax.all_to_all(outgoing[slot], 'grid', split_axis=0, concat_axis=0, tiled...  62.1 us
    reduce_scatter x2, waiting for transfers between devices, body(): lax.psum_scatter(summed, 'grp', scatter_dimension=0, tiled=True)  50.7 us
    pallas_call x2, Pallas kernels, solve_pair(): pl.pallas_call(solve_kernel, in_specs=[pl.BlockSpec(memory_space=pltpu.SM...  21.2 us
    all_to_all x2, waiting for transfers between devices, body(): lax.all_to_all(outgoing[slot], 'grid', split_axis=0, concat_axis=0, tiled...  17.8 us
    all_to_all x1, waiting for transfers between devices, body(): lax.all_to_all(t, 'grid', split_axis=0, concat_axis=0, tiled=True)  14.9 us
    pallas_call x2, Pallas kernels, scatter_pieces(): pl.pallas_call(scatter_kernel, grid_spec=pltpu.PrefetchScalarGridSpec(num...  10.7 us
  transfers between devices with their start and end apart: 7, of which 6 were waited for; matrix products, arithmetic and copies ran while one was open for 1% of the time, Pallas kernels for 9%

profile of v1, /device:TPU:0, one launch (start us, length us, event | category | flops | bytes accessed | tf_op | source)
XLA Modules:
  0.0 387.2 jit_solution(6808570760561516433)
XLA Ops:
  6.5 2.0 copy.29
  8.5 1.6 fusion.4
  10.2 0.7 all-gather.5.cloned.1.call-update
  10.9 0.1 add.33
  11.0 0.1 copy.22
  11.1 0.1 copy.23
  11.2 0.1 compare_reduce_fusion
  11.3 0.2 reduce-window.8
  11.5 0.1 subtract_reduce_fusion
  11.6 0.1 compare_and_fusion
  11.7 0.1 select_reduce_fusion
  11.8 0.1 reshape.127
  12.0 0.1 copy.24
  12.1 0.7 reshape.128.ids_ref
  12.8 52.8 %all-gather.3.cloned.1.call-done.src_ref = f32[64,128,128]{2,1,0:T(8,128)} async-done(((f32[16,128,128]{2,1,0:T(8,128)}), f32[64,128,128]{2,1,0:T(8,128)}) %all-gather.3.cloned.1.call-update) | async-done | bytes 4194320 | tf_op jit(solution)/shard_map/all_gather | solution.py:275
  65.6 5.1 %pick_pieces.2 = (f32[8,2,128,128]{3,2,1,0:T(8,128)}, f32[8,2,128,128]{3,2,1,0:T(8,128)}) custom-call(s32[32]{0:T(128)} %reshape.128.ids_ref, f32[64,128,128]{2,1,0:T(8,128)} %all-gather.3.cloned.1.call-done.src_ref), custom_call_target="tpu_custom_call" | custom-call | bytes 8388608 | tf_op jit(solution)/shard_map/pick_pieces/pallas_call | solution.py:45
  70.7 31.2 %all_to_all.40.refs_0_ = f32[8,2,128,128]{3,2,1,0:T(8,128)S(1)} all-to-all(f32[8,2,128,128]{3,2,1,0:T(8,128)} %get-tuple-element.13), channel_id=1, replica_groups=mesh['grp'=4,'grid'=8] {'grid'}, dimensions={0} | all-to-all | bytes 2097152 | tf_op jit(solution)/shard_map/all_to_all | solution.py:278
  101.8 3.6 all-to-all-start.3
  105.4 14.6 %all-gather.5.cloned.1.call-done.src_ref = f32[64,128,128]{2,1,0:T(8,128)} async-done(((f32[16,128,128]{2,1,0:T(8,128)}), f32[64,128,128]{2,1,0:T(8,128)}) %all-gather.5.cloned.1.call-update) | async-done | bytes 4194320 | tf_op jit(solution)/shard_map/all_gather | solution.py:275
  120.0 5.0 %pick_pieces.3 = (f32[8,2,128,128]{3,2,1,0:T(8,128)}, f32[8,2,128,128]{3,2,1,0:T(8,128)}) custom-call(s32[32]{0:T(128)} %reshape.128.ids_ref, f32[64,128,128]{2,1,0:T(8,128)} %all-gather.5.cloned.1.call-done.src_ref), custom_call_target="tpu_custom_call" | custom-call | bytes 8388608 | tf_op jit(solution)/shard_map/pick_pieces/pallas_call | solution.py:45
  125.1 6.8 %all-to-all-done.3.refs_0_ = f32[8,2,128,128]{3,2,1,0:T(8,128)S(1)} async-done(((f32[8,2,128,128]{3,2,1,0:T(8,128)}), f32[8,2,128,128]{3,2,1,0:T(8,128)S(1)}, u32[]{:S(2)}, u32[]{:S(2)}) %all-to-all-start.3) | async-done | bytes 1048608 | tf_op jit(solution)/shard_map/all_to_all | solution.py:278
  131.9 30.9 %all_to_all.41.refs_1_ = f32[8,2,128,128]{3,2,1,0:T(8,128)} all-to-all(f32[8,2,128,128]{3,2,1,0:T(8,128)} %get-tuple-element.14), channel_id=1, replica_groups=mesh['grp'=4,'grid'=8] {'grid'}, dimensions={0} | all-to-all | bytes 2097152 | tf_op jit(solution)/shard_map/all_to_all | solution.py:278
  162.8 3.6 all-to-all-start.4
  166.4 0.1 copy.26
  166.5 0.1 copy.25
  166.6 0.1 copy.28
  166.7 0.2 fusion.2
  166.9 0.6 gather_fusion.1
  167.4 0.6 gather_fusion
  168.0 0.1 pad_add_fusion
  168.1 1.2 copy-done
  169.3 10.6 %solve_pair.2 = (f32[8,2,128,128]{3,2,1,0:T(8,128)S(1)}, f32[8,2,128,128]{3,2,1,0:T(8,128)S(1)}) custom-call(s32[4]{0:T(128)S(1)} %get-tuple-element.28.info_ref, f32[8,2,128,128]{3,2,1,0:T(8,128)S(1)} %all_to_all.40.refs_0_, f32[8,2,128,128]{3,2,1,0:T(8,128)S(1)} %copy-done), custom_call_target="tpu_custom_call" | custom-call | bytes 41943040 | tf_op jit(solution)/shard_map/solve_pair/pallas_call | solution.py:234
  180.0 0.9 copy-done.1
  180.9 1.0 copy-done.3
  181.9 11.0 %all-to-all-done.4.refs_1_ = f32[8,2,128,128]{3,2,1,0:T(8,128)S(1)} async-done(((f32[8,2,128,128]{3,2,1,0:T(8,128)}), f32[8,2,128,128]{3,2,1,0:T(8,128)S(1)}, u32[]{:S(2)}, u32[]{:S(2)}) %all-to-all-start.4) | async-done | bytes 1048608 | tf_op jit(solution)/shard_map/all_to_all | solution.py:278
  192.8 4.2 %all-to-all-start.6 = ((f32[8,2,128,128]{3,2,1,0:T(8,128)}), f32[8,2,128,128]{3,2,1,0:T(8,128)}, u32[]{:S(2)}, u32[]{:S(2)}) async-start(f32[8,2,128,128]{3,2,1,0:T(8,128)} %copy-done.3), calls=%async_computation.7 | async-start | bytes 2097152 | tf_op jit(solution)/shard_map/all_to_all | solution.py:283
  197.1 10.6 %solve_pair.3 = (f32[8,2,128,128]{3,2,1,0:T(8,128)S(1)}, f32[8,2,128,128]{3,2,1,0:T(8,128)S(1)}) custom-call(s32[4]{0:T(128)S(1)} %get-tuple-element.27.info_ref, f32[8,2,128,128]{3,2,1,0:T(8,128)S(1)} %all-to-all-done.3.refs_0_, f32[8,2,128,128]{3,2,1,0:T(8,128)S(1)} %all-to-all-done.4.refs_1_), custom_call_target="tpu_custom_call" | custom-call | bytes 41943040 | tf_op jit(solution)/shard_map/solve_pair/pallas_call | solution.py:234
  207.8 1.0 copy-done.4
  208.7 14.9 %all-to-all-done.6.refs_0_ = f32[8,2,128,128]{3,2,1,0:T(8,128)} async-done(((f32[8,2,128,128]{3,2,1,0:T(8,128)}), f32[8,2,128,128]{3,2,1,0:T(8,128)}, u32[]{:S(2)}, u32[]{:S(2)}) %all-to-all-start.6) | async-done | bytes 1048608 | tf_op jit(solution)/shard_map/all_to_all | solution.py:283
  223.7 30.8 %all_to_all.42.refs_1_ = f32[8,2,128,128]{3,2,1,0:T(8,128)} all-to-all(f32[8,2,128,128]{3,2,1,0:T(8,128)} %copy-done.4), channel_id=1, replica_groups=mesh['grp'=4,'grid'=8] {'grid'}, dimensions={0} | all-to-all | bytes 2097152 | tf_op jit(solution)/shard_map/all_to_all | solution.py:283
  254.4 5.3 %add_pieces.3 = f32[64,128,128]{2,1,0:T(8,128)} custom-call(s32[32]{0:T(128)} %reshape.128.ids_ref, f32[8,2,128,128]{3,2,1,0:T(8,128)} %all-to-all-done.6.refs_0_, f32[8,2,128,128]{3,2,1,0:T(8,128)} %all_to_all.42.refs_1_), custom_call_target="tpu_custom_call" | custom-call | bytes 8388608 | tf_op jit(solution)/shard_map/add_pieces/pallas_call | solution.py:76
  259.8 1.1 copy-done.2
  261.0 29.7 %all_to_all.43.refs_0_ = f32[8,2,128,128]{3,2,1,0:T(8,128)} all-to-all(f32[8,2,128,128]{3,2,1,0:T(8,128)S(1)} %copy-done.2), channel_id=1, replica_groups=mesh['grp'=4,'grid'=8] {'grid'}, dimensions={0} | all-to-all | bytes 2097152 | tf_op jit(solution)/shard_map/all_to_all | solution.py:283
  290.6 29.7 %all_to_all.44.refs_1_ = f32[8,2,128,128]{3,2,1,0:T(8,128)} all-to-all(f32[8,2,128,128]{3,2,1,0:T(8,128)S(1)} %get-tuple-element.18), channel_id=1, replica_groups=mesh['grp'=4,'grid'=8] {'grid'}, dimensions={0} | all-to-all | bytes 2097152 | tf_op jit(solution)/shard_map/all_to_all | solution.py:283
  320.3 5.4 %add_pieces.2 = f32[64,128,128]{2,1,0:T(8,128)} custom-call(s32[32]{0:T(128)} %reshape.128.ids_ref, f32[8,2,128,128]{3,2,1,0:T(8,128)} %all_to_all.43.refs_0_, f32[8,2,128,128]{3,2,1,0:T(8,128)} %all_to_all.44.refs_1_), custom_call_target="tpu_custom_call" | custom-call | bytes 8388608 | tf_op jit(solution)/shard_map/add_pieces/pallas_call | solution.py:76
  325.8 50.7 %reduce-scatter.3.cloned.1.call-done = f32[16,128,128]{2,1,0:T(8,128)} async-done(((f32[64,128,128]{2,1,0:T(8,128)}), f32[16,128,128]{2,1,0:T(8,128)}) %reduce-scatter.3.cloned.1.call-update) | async-done | bytes 1048592 | tf_op jit(solution)/shard_map/reduce_scatter | solution.py:288
  376.4 1.7 pad_maximum_fusion
  378.1 2.5 copy.32
  (27 shorter events, 0.3 us)
Async XLA Ops:
  6.5 59.1 %all-gather.3.cloned.1.call-start = ((), (), s32[]{:S(2)}) async-start(), calls=%async_computation.10 | async-start | bytes 5242880 | tf_op jit(solution)/shard_map/all_gather | solution.py:275
  10.1 0.9 copy-start.5
  10.1 109.9 %all-gather.5.cloned.1.call-start = ((), (), s32[]{:S(2)}) async-start(), calls=%async_computation.11 | async-start | bytes 5242880 | tf_op jit(solution)/shard_map/all_gather | solution.py:275
  101.8 30.1 %all-to-all-start.3 = ((f32[8,2,128,128]{3,2,1,0:T(8,128)}), f32[8,2,128,128]{3,2,1,0:T(8,128)S(1)}, u32[]{:S(2)}, u32[]{:S(2)}) async-start(f32[8,2,128,128]{3,2,1,0:T(8,128)} %get-tuple-element.16), calls=%async_computation.3 | async-start | bytes 2097152 | tf_op jit(solution)/shard_map/all_to_all | solution.py:278
  131.9 34.5 %copy-start.6 = (s32[64,3]{0,1:T(4,128)S(1)}, s32[64,3]{0,1:T(4,128)}, u32[]{:S(2)}) copy-start(s32[64,3]{0,1:T(4,128)} %param.4) | copy-start | bytes 2308
  162.8 30.1 %all-to-all-start.4 = ((f32[8,2,128,128]{3,2,1,0:T(8,128)}), f32[8,2,128,128]{3,2,1,0:T(8,128)S(1)}, u32[]{:S(2)}, u32[]{:S(2)}) async-start(f32[8,2,128,128]{3,2,1,0:T(8,128)} %get-tuple-element.17), calls=%async_computation.4 | async-start | bytes 2097152 | tf_op jit(solution)/shard_map/all_to_all | solution.py:278
  168.1 1.2 copy-start
  180.0 1.0 copy-start.1
  180.9 1.0 copy-start.3
  192.8 30.8 %all-to-all-start.6 = ((f32[8,2,128,128]{3,2,1,0:T(8,128)}), f32[8,2,128,128]{3,2,1,0:T(8,128)}, u32[]{:S(2)}, u32[]{:S(2)}) async-start(f32[8,2,128,128]{3,2,1,0:T(8,128)} %copy-done.3), calls=%async_computation.7 | async-start | bytes 2097152 | tf_op jit(solution)/shard_map/all_to_all | solution.py:283
  197.1 128.7 %reduce-scatter.5.cloned.1.call-start = ((), (), s32[]{:S(2)}) async-start(), calls=%async_computation.13 | async-start | bytes 5242880 | tf_op jit(solution)/shard_map/reduce_scatter | solution.py:288
  207.8 1.0 copy-start.4
  259.7 1.2 copy-start.2
  259.8 116.7 %reduce-scatter.3.cloned.1.call-start = ((), (), s32[]{:S(2)}) async-start(), calls=%async_computation.12 | async-start | bytes 5242880 | tf_op jit(solution)/shard_map/reduce_scatter | solution.py:288
Sparse Core Ops, SparseCore 0:
  10.2 55.3 all-gather.2
  67.4 52.5 all-gather.4
  259.9 50.5 reduce-scatter.4
  325.9 50.5 reduce-scatter.2

commit v2 on v1

--- a/solution.py
+++ b/solution.py
@@ -250,6 +250,62 @@
     )(info, *parts)
 
 
+def swap_kernel(in_ref, out_ref, send_sems, recv_sems, own_sem):
+    count = in_ref.shape[0]
+    me = lax.axis_index("grid")
+    barrier = pltpu.get_barrier_semaphore()
+    for gap in range(1, count):
+        pl.semaphore_signal(
+            barrier,
+            inc=1,
+            device_id={"grid": lax.rem(me + gap, count)},
+            device_id_type=pl.DeviceIdType.MESH,
+        )
+    pl.semaphore_wait(barrier, count - 1)
+    copies = []
+    for gap in range(1, count):
+        peer = lax.rem(me + gap, count)
+        copy = pltpu.make_async_remote_copy(
+            src_ref=in_ref.at[peer],
+            dst_ref=out_ref.at[me],
+            send_sem=send_sems.at[gap - 1],
+            recv_sem=recv_sems.at[gap - 1],
+            device_id={"grid": peer},
+            device_id_type=pl.DeviceIdType.MESH,
+        )
+        copy.start()
+        copies.append(copy)
+    own = pltpu.make_async_copy(in_ref.at[me], out_ref.at[me], own_sem)
+    own.start()
+    own.wait()
+    for copy in copies:
+        copy.wait()
+
+
+def swap(parts, count):
+    hbm = pl.BlockSpec(memory_space=pl.ANY)
+    return pl.pallas_call(
+        swap_kernel,
+        in_specs=[hbm],
+        out_specs=hbm,
+        out_shape=jax.ShapeDtypeStruct(parts.shape, jnp.float32),
+        scratch_shapes=[
+            pltpu.SemaphoreType.DMA((count - 1,)),
+            pltpu.SemaphoreType.DMA((count - 1,)),
+            pltpu.SemaphoreType.DMA,
+        ],
+        compiler_params=pltpu.CompilerParams(collective_id=0, has_side_effects=True),
+        cost_estimate=pl.CostEstimate(flops=0, bytes_accessed=80 * 1024 * 1024, transcendentals=0),
+        name="swap_pieces",
+    )(parts)
+
+
+def exchange(parts, count, beside):
+    if beside or count > 16:
+        return lax.all_to_all(parts, "grid", split_axis=0, concat_axis=0, tiled=True)
+    return swap(parts, count)
+
+
 def body(orbitals, anchors, pair_slots):
     grid_count = lax.axis_size("grid")
     owner_count = lax.axis_size("grp") * grid_count
@@ -275,12 +331,15 @@
         pieces = lax.all_gather(stacked[:, chunk * rows : (chunk + 1) * rows], "grp", axis=0, tiled=True)
         outgoing = gather_pieces(ids, pieces, slots, grid_count)
         for slot in range(slots):
-            arrived[slot][chunk] = lax.all_to_all(outgoing[slot], "grid", split_axis=0, concat_axis=0, tiled=True)
+            arrived[slot][chunk] = exchange(outgoing[slot], grid_count, slot > 0)
     returned = []
     for slot in range(slots):
         terms = solve_pair(info[slot], arrived[slot])
         returned.append(
-            [lax.all_to_all(t, "grid", split_axis=0, concat_axis=0, tiled=True) for t in terms]
+            [
+                exchange(t, grid_count, slot < slots - 1 and chunk == 0)
+                for chunk, t in enumerate(terms)
+            ]
         )
     results = []
     for chunk in range(chunks):

time: 388 us -> 409 us (1.054)
  Pallas kernels: 42 us -> 203 us
  blocking collectives: 152 us -> 0 us
  starting transfers between devices: 11.5 us -> 19.1 us
  waiting for transfers between devices: 152 us -> 157 us
    pallas_call x0 -> x5, Pallas kernels: none -> 160 us  [swap(): pl.pallas_call(swap_kernel, in_specs=[hbm], out_specs=hbm, out_shape=jax....]
    all_to_all x5 -> x0, blocking collectives: 152 us -> none  [the longest x3 90.1 us: body(): lax.all_to_all(t, 'grid', split_axis=0, concat_axis=0, tiled=True)]
    all_to_all x3, waiting for transfers between devices: 32.7 us -> 0.01 us  [exchange(): lax.all_to_all(parts, 'grid', split_axis=0, concat_axis=0, tiled=True)]
    all_gather x2, waiting for transfers between devices: 67.5 us -> 97.7 us  [body(): lax.all_gather(stacked[:, chunk * rows:(chunk + 1) * rows], 'grp', axis=0...]
    all_to_all x3, starting transfers between devices: 11.4 us -> 19 us  [exchange(): lax.all_to_all(parts, 'grid', split_axis=0, concat_axis=0, tiled=True)]
    reduce_scatter x2, waiting for transfers between devices: 50.7 us -> 58.1 us  [body(): lax.psum_scatter(summed, 'grp', scatter_dimension=0, tiled=True)]
    unnamed x18 -> x20, local copies, waits for them, and re-layouts: 10 us -> 9.84 us
  transfers between devices with their start and end apart: 7 -> 7, of which waited for: 6 -> 4; matrix products, arithmetic and copies ran while one was open for 1% -> 1% of each run, Pallas kernels for 9% -> 39%
where the time goes in v2:
time: 409 us; the launch traced here: 408 us
  Pallas kernels  203 us (50%)
  waiting for transfers between devices  157 us (38%)
  starting transfers between devices  19.1 us (5%)
  local copies, waits for them, and re-layouts  13.7 us (3%)
  between operations  13.4 us (3%)
    pallas_call x5, Pallas kernels, swap(): pl.pallas_call(swap_kernel, in_specs=[hbm], out_specs=hbm, out_shape=jax....  160 us
    all_gather x2, waiting for transfers between devices, body(): lax.all_gather(stacked[:, chunk * rows:(chunk + 1) * rows], 'grp', axis=0...  97.7 us
    reduce_scatter x2, waiting for transfers between devices, body(): lax.psum_scatter(summed, 'grp', scatter_dimension=0, tiled=True)  58.1 us
    pallas_call x2, Pallas kernels, solve_pair(): pl.pallas_call(solve_kernel, in_specs=[pl.BlockSpec(memory_space=pltpu.SM...  22.2 us
    all_to_all x3, starting transfers between devices, exchange(): lax.all_to_all(parts, 'grid', split_axis=0, concat_axis=0, tiled=True)  19 us
    pallas_call x2, Pallas kernels, scatter_pieces(): pl.pallas_call(scatter_kernel, grid_spec=pltpu.PrefetchScalarGridSpec(num...  10.8 us
    pallas_call x2, Pallas kernels, gather_pieces(): pl.pallas_call(gather_kernel, grid_spec=pltpu.PrefetchScalarGridSpec(num_...  10.1 us
    unnamed x20, local copies, waits for them, and re-layouts  9.84 us
  transfers between devices with their start and end apart: 7, of which 4 were waited for; matrix products, arithmetic and copies ran while one was open for 1% of the time, Pallas kernels for 39%

profile of v2, /device:TPU:0, one launch (start us, length us, event | category | flops | bytes accessed | tf_op | source)
XLA Modules:
  0.0 408.4 jit_solution(9999191810353480326)
XLA Ops:
  6.5 2.0 copy.29
  8.5 1.6 fusion.4
  10.1 0.0 all-gather.5.cloned.1.call-start
  10.2 0.7 all-gather.5.cloned.1.call-update
  10.9 0.1 add.33
  11.0 0.1 copy.22
  11.1 0.1 copy.23
  11.2 0.1 compare_reduce_fusion
  11.3 0.2 reduce-window.8
  11.5 0.1 subtract_reduce_fusion
  11.6 0.1 compare_and_fusion
  11.7 0.1 select_reduce_fusion
  11.8 0.1 reshape.127
  12.0 0.1 copy.24
  12.1 0.6 reshape.128.ids_ref
  12.7 52.9 %all-gather.3.cloned.1.call-done.src_ref = f32[64,128,128]{2,1,0:T(8,128)} async-done(((f32[16,128,128]{2,1,0:T(8,128)}), f32[64,128,128]{2,1,0:T(8,128)}) %all-gather.3.cloned.1.call-update) | async-done | bytes 4194320 | tf_op jit(solution)/shard_map/all_gather | solution.py:331
  65.6 5.1 %pick_pieces.2 = (f32[8,2,128,128]{3,2,1,0:T(8,128)}, f32[8,2,128,128]{3,2,1,0:T(8,128)}) custom-call(s32[32]{0:T(128)} %reshape.128.ids_ref, f32[64,128,128]{2,1,0:T(8,128)} %all-gather.3.cloned.1.call-done.src_ref), custom_call_target="tpu_custom_call" | custom-call | bytes 8388608 | tf_op jit(solution)/shard_map/pick_pieces/pallas_call | solution.py:45
  70.7 4.6 %all-to-all-start.1 = ((f32[8,2,128,128]{3,2,1,0:T(8,128)}), f32[8,2,128,128]{3,2,1,0:T(8,128)S(1)}, u32[]{:S(2)}, u32[]{:S(2)}) async-start(f32[8,2,128,128]{3,2,1,0:T(8,128)} %get-tuple-element.16), calls=%async_computation.1 | async-start | bytes 2097152 | tf_op jit(solution)/shard_map/all_to_all | solution.py:305
  75.3 44.8 %all-gather.5.cloned.1.call-done.src_ref = f32[64,128,128]{2,1,0:T(8,128)} async-done(((f32[16,128,128]{2,1,0:T(8,128)}), f32[64,128,128]{2,1,0:T(8,128)}) %all-gather.5.cloned.1.call-update) | async-done | bytes 4194320 | tf_op jit(solution)/shard_map/all_gather | solution.py:331
  120.0 5.0 %pick_pieces.3 = (f32[8,2,128,128]{3,2,1,0:T(8,128)}, f32[8,2,128,128]{3,2,1,0:T(8,128)}) custom-call(s32[32]{0:T(128)} %reshape.128.ids_ref, f32[64,128,128]{2,1,0:T(8,128)} %all-gather.5.cloned.1.call-done.src_ref), custom_call_target="tpu_custom_call" | custom-call | bytes 8388608 | tf_op jit(solution)/shard_map/pick_pieces/pallas_call | solution.py:45
  125.1 4.7 %all-to-all-start.2 = ((f32[8,2,128,128]{3,2,1,0:T(8,128)}), f32[8,2,128,128]{3,2,1,0:T(8,128)S(1)}, u32[]{:S(2)}, u32[]{:S(2)}) async-start(f32[8,2,128,128]{3,2,1,0:T(8,128)} %get-tuple-element.17), calls=%async_computation.2 | async-start | bytes 2097152 | tf_op jit(solution)/shard_map/all_to_all | solution.py:305
  129.9 0.1 copy.26
  130.0 0.1 copy.25
  130.1 0.1 copy.28
  130.2 0.2 fusion.2
  130.4 0.6 gather_fusion.1
  130.9 0.6 gather_fusion
  131.5 0.1 pad_add_fusion
  131.6 39.6 %swap_pieces.6.refs_1_ = f32[8,2,128,128]{3,2,1,0:T(8,128)} custom-call(f32[8,2,128,128]{3,2,1,0:T(8,128)} %get-tuple-element.14.in_ref), custom_call_target="tpu_custom_call" | custom-call | bytes 83886080 | tf_op jit(solution)/shard_map/swap_pieces/pallas_call | solution.py:287
  171.2 26.5 %swap_pieces.5.refs_0_ = f32[8,2,128,128]{3,2,1,0:T(8,128)} custom-call(f32[8,2,128,128]{3,2,1,0:T(8,128)} %get-tuple-element.13.in_ref), custom_call_target="tpu_custom_call" | custom-call | bytes 83886080 | tf_op jit(solution)/shard_map/swap_pieces/pallas_call | solution.py:287
  197.8 1.2 copy-done.1
  199.0 11.6 %solve_pair.2 = (f32[8,2,128,128]{3,2,1,0:T(8,128)}, f32[8,2,128,128]{3,2,1,0:T(8,128)S(1)}) custom-call(s32[4]{0:T(128)S(1)} %get-tuple-element.28.info_ref, f32[8,2,128,128]{3,2,1,0:T(8,128)S(1)} %copy-done.1, f32[8,2,128,128]{3,2,1,0:T(8,128)S(1)} %copy-done), custom_call_target="tpu_custom_call" | custom-call | bytes 41943040 | tf_op jit(solution)/shard_map/solve_pair/pallas_call | solution.py:234
  210.6 1.0 copy-done.3
  211.6 26.3 %swap_pieces.8.refs_0_ = f32[8,2,128,128]{3,2,1,0:T(8,128)} custom-call(f32[8,2,128,128]{3,2,1,0:T(8,128)} %copy-done.3), custom_call_target="tpu_custom_call" | custom-call | bytes 83886080 | tf_op jit(solution)/shard_map/swap_pieces/pallas_call | solution.py:287
  237.9 10.6 %solve_pair.3 = (f32[8,2,128,128]{3,2,1,0:T(8,128)S(1)}, f32[8,2,128,128]{3,2,1,0:T(8,128)S(1)}) custom-call(s32[4]{0:T(128)S(1)} %get-tuple-element.27.info_ref, f32[8,2,128,128]{3,2,1,0:T(8,128)S(1)} %all-to-all-done.1.refs_0_, f32[8,2,128,128]{3,2,1,0:T(8,128)S(1)} %all-to-all-done.2.refs_1_), custom_call_target="tpu_custom_call" | custom-call | bytes 41943040 | tf_op jit(solution)/shard_map/solve_pair/pallas_call | solution.py:234
  248.5 1.0 copy-done.2
  249.4 1.0 copy-done.4
  250.4 26.2 %swap_pieces.9.refs_1_ = f32[8,2,128,128]{3,2,1,0:T(8,128)} custom-call(f32[8,2,128,128]{3,2,1,0:T(8,128)} %copy-done.4), custom_call_target="tpu_custom_call" | custom-call | bytes 83886080 | tf_op jit(solution)/shard_map/swap_pieces/pallas_call | solution.py:287
  276.7 5.3 %add_pieces.3 = f32[64,128,128]{2,1,0:T(8,128)} custom-call(s32[32]{0:T(128)} %reshape.128.ids_ref, f32[8,2,128,128]{3,2,1,0:T(8,128)} %swap_pieces.8.refs_0_, f32[8,2,128,128]{3,2,1,0:T(8,128)} %swap_pieces.9.refs_1_), custom_call_target="tpu_custom_call" | custom-call | bytes 8388608 | tf_op jit(solution)/shard_map/add_pieces/pallas_call | solution.py:76
  282.0 9.7 %all-to-all-start = ((f32[8,2,128,128]{3,2,1,0:T(8,128)}), f32[8,2,128,128]{3,2,1,0:T(8,128)S(1)}, u32[]{:S(2)}, u32[]{:S(2)}) async-start(f32[8,2,128,128]{3,2,1,0:T(8,128)} %get-tuple-element.15), calls=%async_computation | async-start | bytes 2097152 | tf_op jit(solution)/shard_map/all_to_all | solution.py:305
  291.7 0.0 reduce-scatter.3.cloned.1.call-start
  291.7 41.4 %swap_pieces.7.refs_1_ = f32[8,2,128,128]{3,2,1,0:T(8,128)} custom-call(f32[8,2,128,128]{3,2,1,0:T(8,128)} %copy-done.2), custom_call_target="tpu_custom_call" | custom-call | bytes 83886080 | tf_op jit(solution)/shard_map/swap_pieces/pallas_call | solution.py:287
  333.1 1.0 copy-done.5
  334.1 5.4 %add_pieces.2 = f32[64,128,128]{2,1,0:T(8,128)} custom-call(s32[32]{0:T(128)} %reshape.128.ids_ref, f32[8,2,128,128]{3,2,1,0:T(8,128)} %copy-done.5, f32[8,2,128,128]{3,2,1,0:T(8,128)} %swap_pieces.7.refs_1_), custom_call_target="tpu_custom_call" | custom-call | bytes 8388608 | tf_op jit(solution)/shard_map/add_pieces/pallas_call | solution.py:76
  339.6 0.3 reduce-scatter.5.cloned.1.call-done
  339.9 57.8 %reduce-scatter.3.cloned.1.call-done = f32[16,128,128]{2,1,0:T(8,128)} async-done(((f32[64,128,128]{2,1,0:T(8,128)}), f32[16,128,128]{2,1,0:T(8,128)}) %reduce-scatter.3.cloned.1.call-update) | async-done | bytes 1048592 | tf_op jit(solution)/shard_map/reduce_scatter | solution.py:347
  397.7 1.7 pad_maximum_fusion
  399.4 2.5 copy.32
  (29 shorter events, 0.2 us)
Async XLA Ops:
  6.5 59.1 %all-gather.3.cloned.1.call-start = ((), (), s32[]{:S(2)}) async-start(), calls=%async_computation.5 | async-start | bytes 5242880 | tf_op jit(solution)/shard_map/all_gather | solution.py:331
  10.1 0.9 copy-start.6
  10.1 109.9 %all-gather.5.cloned.1.call-start = ((), (), s32[]{:S(2)}) async-start(), calls=%async_computation.6 | async-start | bytes 5242880 | tf_op jit(solution)/shard_map/all_gather | solution.py:331
  70.7 54.4 %all-to-all-start.1 = ((f32[8,2,128,128]{3,2,1,0:T(8,128)}), f32[8,2,128,128]{3,2,1,0:T(8,128)S(1)}, u32[]{:S(2)}, u32[]{:S(2)}) async-start(f32[8,2,128,128]{3,2,1,0:T(8,128)} %get-tuple-element.16), calls=%async_computation.1 | async-start | bytes 2097152 | tf_op jit(solution)/shard_map/all_to_all | solution.py:305
  125.1 4.8 %copy-start.7 = (s32[64,3]{0,1:T(4,128)S(1)}, s32[64,3]{0,1:T(4,128)}, u32[]{:S(2)}) copy-start(s32[64,3]{0,1:T(4,128)} %param.4) | copy-start | bytes 2308
  125.1 112.8 %all-to-all-start.2 = ((f32[8,2,128,128]{3,2,1,0:T(8,128)}), f32[8,2,128,128]{3,2,1,0:T(8,128)S(1)}, u32[]{:S(2)}, u32[]{:S(2)}) async-start(f32[8,2,128,128]{3,2,1,0:T(8,128)} %get-tuple-element.17), calls=%async_computation.2 | async-start | bytes 2097152 | tf_op jit(solution)/shard_map/all_to_all | solution.py:305
  129.8 210.1 %reduce-scatter.5.cloned.1.call-start = ((), (), s32[]{:S(2)}) async-start(), calls=%async_computation.8 | async-start | bytes 5242880 | tf_op jit(solution)/shard_map/reduce_scatter | solution.py:347
  171.2 26.5 %copy-start = (f32[8,2,128,128]{3,2,1,0:T(8,128)S(1)}, f32[8,2,128,128]{3,2,1,0:T(8,128)}, u32[]{:S(2)}) copy-start(f32[8,2,128,128]{3,2,1,0:T(8,128)} %swap_pieces.6.refs_1_) | copy-start | bytes 3145732
  197.8 1.2 copy-start.1
  210.6 1.0 copy-start.3
  248.5 1.0 copy-start.2
  249.4 1.0 copy-start.4
  282.0 51.1 %all-to-all-start = ((f32[8,2,128,128]{3,2,1,0:T(8,128)}), f32[8,2,128,128]{3,2,1,0:T(8,128)S(1)}, u32[]{:S(2)}, u32[]{:S(2)}) async-start(f32[8,2,128,128]{3,2,1,0:T(8,128)} %get-tuple-element.15), calls=%async_computation | async-start | bytes 2097152 | tf_op jit(solution)/shard_map/all_to_all | solution.py:305
  291.7 106.0 %reduce-scatter.3.cloned.1.call-start = ((), (), s32[]{:S(2)}) async-start(), calls=%async_computation.7 | async-start | bytes 5242880 | tf_op jit(solution)/shard_map/reduce_scatter | solution.py:347
  333.1 1.0 copy-start.5
Sparse Core Ops, SparseCore 0:
  10.2 55.3 all-gather.2
  67.4 52.5 all-gather.4
  282.1 57.6 reduce-scatter.4
  342.7 54.9 reduce-scatter.2
